TPU v7x, 32 devices: a whole 2x2x4 slice. The times are simulated.
32 devices in a mesh: seq: 16 (over z, y, x), bat: 2 (over core).
Axes of the slice: x: 2, y: 2, z: 4, core: 2. Of those that a mesh axis runs over, the one named last changes fastest.
Arguments:
- tokens: bfloat16 [2, 65536, 256], P('bat', 'seq'), may hold values from -6 to 6
- filter_spectrum: bfloat16 [2, 256, 256, 256], P(None, 'seq', None, 'bat'), may hold values from -6 to 6
- skip_gain: float32 [256], replicated, may hold values from 0.5 to 1.5
Outputs:
- mixed: bfloat16 [2, 65536, 256], P('bat', 'seq')
All inputs are finite; a program needn't handle non-finite values.
Results may differ from a plain program's by a relative error of at most 0.012.
Values may be sent and summed in bfloat16 or wider, within the bound.
A program may use at most 64 MiB of HBM per device.

v0:
```python
import math

import jax
import jax.numpy as jnp
from jax import lax
from jax.sharding import PartitionSpec as P

N1 = 256
N2 = 256


def cos_sin(points):
    steps_range = jnp.arange(points, dtype=jnp.int32)
    index_grid = steps_range[:, None] * steps_range[None, :] % points
    phase_angle = index_grid.astype(jnp.float32) * (2.0 * math.pi / points)
    return (jnp.cos(phase_angle), jnp.sin(phase_angle))


def real_table(points):
    cosine, sine_vals = cos_sin(points)
    return jnp.stack([cosine, -sine_vals], axis=1).astype(jnp.bfloat16)


def complex_table(points, signum, factor):
    cosine, sine_vals = cos_sin(points)
    top_rows = jnp.stack([cosine, signum * sine_vals], axis=1)
    low_rows = jnp.stack([-signum * sine_vals, cosine], axis=1)
    return (jnp.stack([top_rows, low_rows], axis=0) * factor).astype(jnp.bfloat16)


def final_table(points):
    cosine, sine_vals = cos_sin(points)
    return (jnp.stack([cosine, -sine_vals], axis=0) / points).astype(jnp.bfloat16)


def twiddle_phase(first_rows, second_rows, period):
    index_grid = first_rows[:, None] * second_rows[None, :] % period
    phase_angle = index_grid.astype(jnp.float32) * (2.0 * math.pi / period)
    return (jnp.cos(phase_angle)[..., None], jnp.sin(phase_angle)[..., None])


def multiply(values, filters):
    chosen = values.astype(jnp.float32)
    weights = lax.all_gather(filters, "bat", axis=3, tiled=True).astype(jnp.float32)[:, None]
    real_part = chosen[0] * weights[0] - chosen[1] * weights[1]
    imag_part = chosen[0] * weights[1] + chosen[1] * weights[0]
    return jnp.stack([real_part, imag_part]).astype(jnp.bfloat16)


def body(tokens, filter_spectrum, skip_gain):
    seq_count = lax.axis_size("seq")
    device_index = lax.axis_index("seq")
    batch_rows, local_length, channels = tokens.shape
    rows_local = N1 // seq_count
    cols_local = N2 // seq_count
    period = N1 * N2
    laid_out = tokens.reshape(batch_rows, rows_local, N2, channels)
    columns = lax.all_to_all(laid_out, "seq", split_axis=2, concat_axis=1, tiled=True)
    first_section = jnp.einsum(
        "bnmc,nsk->sbkmc", columns, real_table(N1), preferred_element_type=jnp.float32
    )
    own_cols = device_index * cols_local + jnp.arange(cols_local, dtype=jnp.int32)
    cos_tw, sin_tw = twiddle_phase(jnp.arange(N1, dtype=jnp.int32), own_cols, period)
    real_part = first_section[0] * cos_tw + first_section[1] * sin_tw
    imag_part = first_section[1] * cos_tw - first_section[0] * sin_tw
    turned = jnp.stack([real_part, imag_part]).astype(jnp.bfloat16)
    rows_block = lax.all_to_all(turned, "seq", split_axis=2, concat_axis=3, tiled=True)
    spectrum = jnp.einsum(
        "rbknc,rnsj->sbkjc",
        rows_block,
        complex_table(N2, -1.0, 1.0),
        preferred_element_type=jnp.float32,
    ).astype(jnp.bfloat16)
    product = multiply(spectrum, filter_spectrum)
    back_section = jnp.einsum(
        "rbkjc,rjsn->sbknc",
        product,
        complex_table(N2, 1.0, 1.0 / N2),
        preferred_element_type=jnp.float32,
    )
    own_rows = device_index * rows_local + jnp.arange(rows_local, dtype=jnp.int32)
    cos_back, sin_back = twiddle_phase(own_rows, jnp.arange(N2, dtype=jnp.int32), period)
    real_back = back_section[0] * cos_back - back_section[1] * sin_back
    imag_back = back_section[0] * sin_back + back_section[1] * cos_back
    turned_back = jnp.stack([real_back, imag_back]).astype(jnp.bfloat16)
    mixed_cols = lax.all_to_all(turned_back, "seq", split_axis=3, concat_axis=2, tiled=True)
    filtered = jnp.einsum(
        "rbknc,rkm->bmnc", mixed_cols, final_table(N1), preferred_element_type=jnp.float32
    )
    result = (filtered + skip_gain * columns.astype(jnp.float32)).astype(jnp.bfloat16)
    restored = lax.all_to_all(result, "seq", split_axis=1, concat_axis=2, tiled=True)
    return restored.reshape(batch_rows, local_length, channels)


def solution(mesh):
    placed = (P("bat", "seq", None), P(None, "seq", None, "bat"), P())
    return jax.shard_map(
        body, mesh=mesh, in_specs=placed, out_specs=P("bat", "seq", None), check_vma=False
    )
```

profile of v0, /device:TPU:0, one launch (start us, length us, event | category | flops | bytes accessed | tf_op | source)
XLA Modules:
  0.0 355.4 jit_solution(5459308199365572002)
XLA Ops:
  6.5 4.1 %copy.31 = bf16[1,16,256,256]{3,1,0,2:T(8,128)(2,1)} copy(bf16[1,16,256,256]{3,2,1,0:T(8,128)(2,1)} %bitcast.109) | data formatting | bytes 4194304 | tf_op jit(solution)/shard_map/reshape | solution.py:57
  10.6 8.3 %all-to-all-start = ((bf16[1,16,256,256]{3,1,0,2:T(8,128)(2,1)}), bf16[1,16,256,256]{3,1,0,2:T(8,128)(2,1)S(1)}, u32[]{:S(2)}, u32[]{:S(2)}) async-start(bf16[1,16,256,256]{3,1,0,2:T(8,128)(2,1)} %copy.31), calls=%async_computation | async-start | bytes 4194304 | tf_op jit(solution)/shard_map/all_to_all | solution.py:58
  19.0 1.1 negate_convert_fusion
  20.1 0.2 fusion.57
  20.2 41.8 %all-to-all-done = bf16[1,16,256,256]{3,1,0,2:T(8,128)(2,1)S(1)} async-done(((bf16[1,16,256,256]{3,1,0,2:T(8,128)(2,1)}), bf16[1,16,256,256]{3,1,0,2:T(8,128)(2,1)S(1)}, u32[]{:S(2)}, u32[]{:S(2)}) %all-to-all-start) | async-done | bytes 2097184 | tf_op jit(solution)/shard_map/all_to_all | solution.py:58
  62.0 0.7 copy.32
  62.7 1.2 copy.33
  63.9 1.3 fusion.18
  65.2 1.5 fusion.8
  66.6 0.4 pad_maximum_fusion
  67.0 4.3 %copy.34 = bf16[2,1,256,16,256]{4,3,1,0,2:T(8,128)(2,1)} copy(bf16[2,1,256,16,256]{4,2,3,1,0:T(8,128)(2,1)S(1)} %pad_maximum_fusion) | data formatting | bytes 8388608 | tf_op jit(solution)/shard_map/stack | solution.py:66
  71.3 10.1 %all-to-all-start.1 = ((bf16[2,1,256,16,256]{4,3,1,0,2:T(8,128)(2,1)}), bf16[2,1,256,16,256]{4,3,1,0,2:T(8,128)(2,1)}, u32[]{:S(2)}, u32[]{:S(2)}) async-start(bf16[2,1,256,16,256]{4,3,1,0,2:T(8,128)(2,1)} %copy.34), calls=%async_computation.1 | async-start | bytes 8388608 | tf_op jit(solution)/shard_map/all_to_all | solution.py:67
  81.4 0.2 all-gather.2.cloned.1.call-start
  81.6 0.5 all-gather.2.cloned.1.call-update
  82.1 1.0 fusion.38
  83.1 1.0 fusion.37
  84.1 1.0 broadcast_multiply_fusion
  85.1 0.1 fusion.16
  85.1 0.9 maximum_bitcast_fusion
  86.0 0.2 fusion.55
  86.2 11.6 %all-gather.2.cloned.1.call-done = bf16[2,16,256,256]{3,2,1,0:T(8,128)(2,1)} async-done(((bf16[2,16,256,128]{3,2,1,0:T(8,128)(2,1)}), bf16[2,16,256,256]{3,2,1,0:T(8,128)(2,1)}) %all-gather.2.cloned.1.call-update) | async-done | bytes 4194320 | tf_op jit(solution)/shard_map/all_gather | solution.py:44
  97.8 6.5 %convert_element_type.144 = f32[2,16,256,256]{3,2,1,0:T(8,128)} convert(bf16[2,16,256,256]{3,2,1,0:T(8,128)(2,1)} %all-gather.2.cloned.1.call-done) | non-fusion elementwise | flops 2097152 | bytes 12582912 | tf_op jit(solution)/shard_map/convert_element_type | solution.py:44
  104.3 55.5 %all-to-all-done.1 = bf16[2,1,256,16,256]{4,3,1,0,2:T(8,128)(2,1)} async-done(((bf16[2,1,256,16,256]{4,3,1,0,2:T(8,128)(2,1)}), bf16[2,1,256,16,256]{4,3,1,0,2:T(8,128)(2,1)}, u32[]{:S(2)}, u32[]{:S(2)}) %all-to-all-start.1) | async-done | bytes 4194336 | tf_op jit(solution)/shard_map/all_to_all | solution.py:67
  159.8 2.7 copy.35
  162.5 0.0 slice-start
  162.5 0.0 slice-start.1
  162.5 2.4 convert_bitcast_fusion.1
  164.9 0.0 slice-done
  164.9 1.1 slice-done.1
  166.0 0.0 copy-start
  166.0 1.8 subtract_convert_fusion.1
  167.8 0.0 copy-done
  167.8 2.4 fusion.5
  170.2 1.5 subtract_convert_fusion
  171.6 0.4 pad_maximum_fusion.2
  172.0 4.4 %copy.40 = bf16[2,1,16,256,256]{4,2,0,1,3:T(8,128)(2,1)} copy(bf16[2,1,16,256,256]{4,3,2,0,1:T(8,128)(2,1)S(1)} %pad_maximum_fusion.2) | data formatting | bytes 8388608 | tf_op jit(solution)/shard_map/stack | solution.py:85
  176.4 19.4 %all-to-all-start.2 = ((bf16[2,1,16,256,256]{4,2,0,1,3:T(8,128)(2,1)}), bf16[2,1,16,256,256]{4,2,0,1,3:T(8,128)(2,1)}, u32[]{:S(2)}, u32[]{:S(2)}) async-start(bf16[2,1,16,256,256]{4,2,0,1,3:T(8,128)(2,1)} %copy.40), calls=%async_computation.2 | async-start | bytes 8388608 | tf_op jit(solution)/shard_map/all_to_all | solution.py:86
  195.8 1.0 sine_negate_fusion
  196.9 77.4 %all-to-all-done.2 = bf16[2,1,16,256,256]{4,2,0,1,3:T(8,128)(2,1)} async-done(((bf16[2,1,16,256,256]{4,2,0,1,3:T(8,128)(2,1)}), bf16[2,1,16,256,256]{4,2,0,1,3:T(8,128)(2,1)}, u32[]{:S(2)}, u32[]{:S(2)}) %all-to-all-start.2) | async-done | bytes 4194336 | tf_op jit(solution)/shard_map/all_to_all | solution.py:86
  274.3 0.0 copy-start.1
  274.3 2.7 copy.41
  277.0 0.0 copy-done.1
  277.0 1.3 fusion.10
  278.4 1.2 copy.42
  279.6 67.4 %all_to_all.60 = bf16[1,256,16,256]{3,2,0,1:T(8,128)(2,1)S(1)} all-to-all(bf16[1,256,16,256]{3,2,0,1:T(8,128)(2,1)S(1)} %copy.42), channel_id=1, replica_groups=mesh['seq'=16,'bat'=2] {'seq'}, dimensions={1} | all-to-all | bytes 4194304 | tf_op jit(solution)/shard_map/all_to_all | solution.py:91
  347.0 1.5 copy.43
  (2 shorter events, 0.0 us)
Async XLA Ops:
  10.6 51.4 %all-to-all-start = ((bf16[1,16,256,256]{3,1,0,2:T(8,128)(2,1)}), bf16[1,16,256,256]{3,1,0,2:T(8,128)(2,1)S(1)}, u32[]{:S(2)}, u32[]{:S(2)}) async-start(bf16[1,16,256,256]{3,1,0,2:T(8,128)(2,1)} %copy.31), calls=%async_computation | async-start | bytes 4194304 | tf_op jit(solution)/shard_map/all_to_all | solution.py:58
  71.3 88.5 %all-to-all-start.1 = ((bf16[2,1,256,16,256]{4,3,1,0,2:T(8,128)(2,1)}), bf16[2,1,256,16,256]{4,3,1,0,2:T(8,128)(2,1)}, u32[]{:S(2)}, u32[]{:S(2)}) async-start(bf16[2,1,256,16,256]{4,3,1,0,2:T(8,128)(2,1)} %copy.34), calls=%async_computation.1 | async-start | bytes 8388608 | tf_op jit(solution)/shard_map/all_to_all | solution.py:67
  81.4 16.4 %all-gather.2.cloned.1.call-start = ((), (), s32[]{:S(2)}) async-start(), calls=%async_computation.4 | async-start | bytes 6291456 | tf_op jit(solution)/shard_map/all_gather | solution.py:44
  162.5 2.4 slice-start
  162.5 3.5 slice-start.1
  166.0 1.8 copy-start
  176.4 97.9 %all-to-all-start.2 = ((bf16[2,1,16,256,256]{4,2,0,1,3:T(8,128)(2,1)}), bf16[2,1,16,256,256]{4,2,0,1,3:T(8,128)(2,1)}, u32[]{:S(2)}, u32[]{:S(2)}) async-start(bf16[2,1,16,256,256]{4,2,0,1,3:T(8,128)(2,1)} %copy.40), calls=%async_computation.2 | async-start | bytes 8388608 | tf_op jit(solution)/shard_map/all_to_all | solution.py:86
  274.3 2.8 copy-start.1
Sparse Core Ops, SparseCore 0:
  83.7 13.9 all-gather.1
where the time goes:
time: 356 us; the launch traced here: 355 us
  waiting for transfers between devices  187 us (53%)
  blocking collectives  67.4 us (19%)
  starting transfers between devices  38 us (11%)
  local copies, waits for them, and re-layouts  24 us (7%)
  other arithmetic  18.3 us (5%)
  between operations  13.6 us (4%)
  matrix products  7.29 us (2%)
    all_to_all x1, waiting for transfers between devices, body(): lax.all_to_all(turned_back, 'seq', split_axis=3, concat_axis=2, tiled=True)  77.4 us
    all_to_all x1, blocking collectives, body(): lax.all_to_all(result, 'seq', split_axis=1, concat_axis=2, tiled=True)  67.4 us
    all_to_all x1, waiting for transfers between devices, body(): lax.all_to_all(turned, 'seq', split_axis=2, concat_axis=3, tiled=True)  55.5 us
    all_to_all x1, waiting for transfers between devices, body(): lax.all_to_all(laid_out, 'seq', split_axis=2, concat_axis=1, tiled=True)  41.8 us
    all_to_all x1, starting transfers between devices, body(): lax.all_to_all(turned_back, 'seq', split_axis=3, concat_axis=2, tiled=True)  19.4 us
    all_gather x1, waiting for transfers between devices, multiply(): lax.all_gather(filters, 'bat', axis=3, tiled=True).astype(jnp.float32)  11.6 us
    all_to_all x1, starting transfers between devices, body(): lax.all_to_all(turned, 'seq', split_axis=2, concat_axis=3, tiled=True)  10.1 us
    all_to_all x1, starting transfers between devices, body(): lax.all_to_all(laid_out, 'seq', split_axis=2, concat_axis=1, tiled=True)  8.34 us
  transfers between devices with their start and end apart: 4, of which 4 were waited for; matrix products, arithmetic and copies ran while one was open for 4% of the time, Pallas kernels for 0%

commit v1 on v0

v1 whole, which is shorter than its diff:
```python
import functools

import jax
import jax.numpy as jnp
import numpy as np
from jax import lax
from jax.experimental import pallas as pl
from jax.experimental.pallas import tpu as pltpu
from jax.sharding import PartitionSpec as P


def cos_sin(points):
    grid = np.outer(np.arange(points), np.arange(points)) % points
    angle = grid * (2.0 * np.pi / points)
    return np.cos(angle), np.sin(angle)


def tables(n1, n2):
    cos1, sin1 = cos_sin(n1)
    cos2, sin2 = cos_sin(n2)
    first = np.concatenate([cos1, -sin1], axis=0)
    forward = np.block([[cos2, -sin2], [sin2, cos2]])
    back = np.block([[cos2, sin2], [-sin2, cos2]]) / n2
    last = np.concatenate([cos1, -sin1], axis=1) / n1
    theta = np.outer(np.arange(n1), np.arange(n2)) % (n1 * n2) * (2.0 * np.pi / (n1 * n2))
    half = [t.astype(np.float32).astype(jnp.bfloat16) for t in (first, forward, back, last)]
    turn = np.stack([np.cos(theta), np.sin(theta)]).astype(np.float32)
    return (*half, turn)


def convolve(tile, filt_re, filt_im, gain, first, forward, back, last, turn):
    f32, bf16 = jnp.float32, jnp.bfloat16
    n1, n2 = tile.shape
    dot = functools.partial(jnp.dot, preferred_element_type=f32)
    section = dot(first, tile)
    cos_t, sin_t = turn[0], turn[1]
    a_re, a_im = section[:n1], section[n1:]
    turned = jnp.concatenate(
        [(a_re * cos_t + a_im * sin_t).astype(bf16), (a_im * cos_t - a_re * sin_t).astype(bf16)],
        axis=1,
    )
    spectrum = dot(turned, forward).astype(bf16).astype(f32)
    x_re, x_im = spectrum[:, :n2], spectrum[:, n2:]
    f_re, f_im = filt_re.astype(f32), filt_im.astype(f32)
    product = jnp.concatenate(
        [(x_re * f_re - x_im * f_im).astype(bf16), (x_re * f_im + x_im * f_re).astype(bf16)],
        axis=1,
    )
    section = dot(product, back)
    b_re, b_im = section[:, :n2], section[:, n2:]
    turned = jnp.concatenate(
        [(b_re * cos_t - b_im * sin_t).astype(bf16), (b_re * sin_t + b_im * cos_t).astype(bf16)],
        axis=0,
    )
    filtered = dot(last, turned)
    return (filtered + gain * tile.astype(f32)).astype(bf16)


def kernel(tok_ref, filt_ref, gain_ref, first, forward, back, last, turn, out_ref):
    devs, _, rows, n2 = tok_ref.shape
    n1 = devs * rows
    tile = tok_ref[:, 0].reshape(n1, n2)
    filt_re = filt_ref[:, 0, 0].reshape(n1, n2)
    filt_im = filt_ref[:, 0, 1].reshape(n1, n2)
    gain = gain_ref[pl.program_id(0)]
    out = convolve(
        tile, filt_re, filt_im, gain, first[...], forward[...], back[...], last[...], turn[...]
    )
    out_ref[...] = out.reshape(devs, 1, rows, n2)


def body(tokens, filter_spectrum, skip_gain):
    seq = lax.axis_size("seq")
    bats = lax.axis_size("bat")
    me, bat = lax.axis_index("seq"), lax.axis_index("bat")
    sequences, local, channels = tokens.shape
    _, rows, n2, held = filter_spectrum.shape
    n1 = rows * seq
    consts = tables(n1, n2)
    mine = channels // seq
    if sequences == 1 and bats == 2 and held % seq == 0 and rows % 16 == 0:
        part = held // seq
        tok = tokens[0].T.reshape(bats, seq, part, rows, n2).transpose(1, 0, 2, 3, 4)
        tok = tok.reshape(seq, mine, rows, n2)
        fil = filter_spectrum.transpose(3, 0, 1, 2).reshape(seq, part, 2, rows, n2)
        fil = lax.all_to_all(fil, "seq", split_axis=0, concat_axis=0)
        tok = lax.all_to_all(tok, "seq", split_axis=0, concat_axis=0)
        other = lax.ppermute(fil, "bat", [(0, 1), (1, 0)])
        low = jnp.where(bat == 0, fil, other)
        high = jnp.where(bat == 0, other, fil)
        fil = jnp.concatenate([low, high], axis=1)
        gain = lax.dynamic_slice_in_dim(skip_gain.reshape(bats, seq, part), me, 1, axis=1)
        gain = gain.reshape(mine)
        whole = lambda t: pl.BlockSpec(t.shape, lambda c: (0,) * t.ndim)
        out = pl.pallas_call(
            kernel,
            grid=(mine,),
            in_specs=[
                pl.BlockSpec((seq, 1, rows, n2), lambda c: (0, c, 0, 0)),
                pl.BlockSpec((seq, 1, 2, rows, n2), lambda c: (0, c, 0, 0, 0)),
                pl.BlockSpec(memory_space=pltpu.SMEM),
                *[whole(t) for t in consts],
            ],
            out_specs=pl.BlockSpec((seq, 1, rows, n2), lambda c: (0, c, 0, 0)),
            out_shape=jax.ShapeDtypeStruct((seq, mine, rows, n2), jnp.bfloat16),
        )(tok, fil, gain, *[jnp.asarray(t) for t in consts])
        out = lax.all_to_all(out, "seq", split_axis=0, concat_axis=0)
        out = out.reshape(seq, bats, part, local).transpose(1, 0, 2, 3).reshape(channels, local)
        return out.T[None]
    fil = lax.all_gather(filter_spectrum, "bat", axis=3, tiled=True).transpose(0, 3, 1, 2)
    fil = lax.all_to_all(fil, "seq", split_axis=1, concat_axis=2, tiled=True)
    tok = tokens.reshape(sequences, rows, n2, channels).transpose(0, 3, 1, 2)
    tok = lax.all_to_all(tok, "seq", split_axis=1, concat_axis=2, tiled=True)
    gain = lax.dynamic_slice_in_dim(skip_gain, me * mine, mine)
    one = lambda t, f, g: convolve(t, f[0], f[1], g, *[jnp.asarray(t) for t in consts])
    per_channel = jax.vmap(one, in_axes=(0, 1, 0))
    out = jax.vmap(per_channel, in_axes=(0, None, None))(tok, fil, gain)
    out = lax.all_to_all(out, "seq", split_axis=2, concat_axis=1, tiled=True)
    return out.reshape(sequences, channels, local).transpose(0, 2, 1)


def solution(mesh):
    placed = (P("bat", "seq", None), P(None, "seq", None, "bat"), P())
    return jax.shard_map(
        body, mesh=mesh, in_specs=placed, out_specs=P("bat", "seq", None), check_vma=False
    )
```

time: 356 us -> 195 us (0.55)
  waiting for transfers between devices: 187 us -> 75 us
  Pallas kernels: 0 us -> 19.5 us
  starting transfers between devices: 38 us -> 18.6 us
  between operations: 13.6 us -> 0.06 us
  other arithmetic: 18.3 us -> 4.79 us
  blocking collectives: 67.4 us -> 58 us
  matrix products: 7.29 us -> 0 us
  local copies, waits for them, and re-layouts: 24 us -> 18 us
    all_to_all x3 -> x2, waiting for transfers between devices: 175 us -> 71.3 us  [the longest x1 38.2 us: body(): fil = lax.all_to_all(fil, 'seq', split_axis=0, concat_axis=0)]
    pallas_call x0 -> x1, Pallas kernels: none -> 19.5 us  [body(): pl.pallas_call(kernel, grid=(mine,), in_specs=[pl.BlockSpec((seq, 1, rows...]
    all_to_all x3 -> x2, starting transfers between devices: 37.8 us -> 18.5 us  [the longest x1 10.1 us: body(): tok = lax.all_to_all(tok, 'seq', split_axis=0, concat_axis=0)]
    all_gather x1 -> x0, waiting for transfers between devices: 11.6 us -> none  [multiply(): lax.all_gather(filters, 'bat', axis=3, tiled=True).astype(jnp.float32)]
    transpose x0 -> x3, local copies, waits for them, and re-layouts: none -> 9.44 us  [the longest x2 4.89 us: body(): tokens[0].T.reshape(bats, seq, part, rows, n2).transpose(1, 0, 2, 3, 4)]
    all_to_all x1, blocking collectives: 67.4 us -> 58 us  [body(): out = lax.all_to_all(out, 'seq', split_axis=0, concat_axis=0)]
    all_to_all x5 -> x0, local copies, waits for them, and re-layouts: 8.92 us -> none  [the longest x1 2.75 us: body(): lax.all_to_all(turned_back, 'seq', split_axis=3, concat_axis=2, tiled=True)]
    another operation x2 -> x0, local copies, waits for them, and re-layouts: 8.71 us -> none  [the longest x1 4.4 us: body(): turned_back = jnp.stack([real_back, imag_back]).astype(jnp.bfloat16)]
  transfers between devices with their start and end apart: 4 -> 3, of which waited for: 4 -> 3; matrix products, arithmetic and copies ran while one was open for 4% -> 5% of each run, Pallas kernels for 0% -> 0%
where the time goes in v1:
time: 195 us; the launch traced here: 194 us
  waiting for transfers between devices  75 us (38%)
  blocking collectives  58 us (30%)
  Pallas kernels  19.5 us (10%)
  starting transfers between devices  18.6 us (10%)
  local copies, waits for them, and re-layouts  18 us (9%)
  other arithmetic  4.79 us (2%)
    all_to_all x1, blocking collectives, body(): out = lax.all_to_all(out, 'seq', split_axis=0, concat_axis=0)  58 us
    all_to_all x1, waiting for transfers between devices, body(): fil = lax.all_to_all(fil, 'seq', split_axis=0, concat_axis=0)  38.2 us
    all_to_all x1, waiting for transfers between devices, body(): tok = lax.all_to_all(tok, 'seq', split_axis=0, concat_axis=0)  33.1 us
    pallas_call x1, Pallas kernels, body(): pl.pallas_call(kernel, grid=(mine,), in_specs=[pl.BlockSpec((seq, 1, rows...  19.5 us
    all_to_all x1, starting transfers between devices, body(): tok = lax.all_to_all(tok, 'seq', split_axis=0, concat_axis=0)  10.1 us
    all_to_all x1, starting transfers between devices, body(): fil = lax.all_to_all(fil, 'seq', split_axis=0, concat_axis=0)  8.39 us
    transpose x2, local copies, waits for them, and re-layouts, body(): tokens[0].T.reshape(bats, seq, part, rows, n2).transpose(1, 0, 2, 3, 4)  4.89 us
    transpose x1, local copies, waits for them, and re-layouts, body(): fil = filter_spectrum.transpose(3, 0, 1, 2).reshape(seq, part, 2, rows, n2)  4.56 us
  transfers between devices with their start and end apart: 3, of which 3 were waited for; matrix products, arithmetic and copies ran while one was open for 5% of the time, Pallas kernels for 0%

profile of v1, /device:TPU:0, one launch (start us, length us, event | category | flops | bytes accessed | tf_op | source)
XLA Modules:
  0.0 194.0 jit_solution(8716659094780239116)
XLA Ops:
  0.0 4.6 %copy.14 = bf16[128,2,16,256]{3,2,1,0:T(8,128)(2,1)} copy(bf16[128,2,16,256]{0,3,2,1:T(8,128)(2,1)} %bitcast.24) | data formatting | bytes 4194304 | tf_op jit(solution)/shard_map/transpose | solution.py:85
  4.6 8.4 %all-to-all-start.1 = ((bf16[16,8,2,16,256]{4,3,2,1,0:T(8,128)(2,1)}), bf16[16,8,2,16,256]{4,3,2,1,0:T(8,128)(2,1)}, u32[]{:S(2)}, u32[]{:S(2)}) async-start(bf16[16,8,2,16,256]{4,3,2,1,0:T(8,128)(2,1)} %bitcast.5), calls=%async_computation.1 | async-start | bytes 4194304 | tf_op jit(solution)/shard_map/all_to_all | solution.py:86
  13.0 2.9 %copy.12 = bf16[256,4096]{1,0:T(8,128)(2,1)S(1)} copy(bf16[256,4096]{0,1:T(8,128)(2,1)} %bitcast.25) | data formatting | bytes 4194304 | tf_op jit(solution)/shard_map/transpose | solution.py:83
  15.9 2.0 %copy.13 = bf16[16,2,8,16,256]{4,3,2,1,0:T(8,128)(2,1)} copy(bf16[16,2,8,16,256]{4,2,3,0,1:T(8,128)(2,1)S(1)} %bitcast.23) | data formatting | bytes 4194304 | tf_op jit(solution)/shard_map/transpose | solution.py:83
  17.9 38.2 %all-to-all-done.1 = bf16[16,8,2,16,256]{4,3,2,1,0:T(8,128)(2,1)} async-done(((bf16[16,8,2,16,256]{4,3,2,1,0:T(8,128)(2,1)}), bf16[16,8,2,16,256]{4,3,2,1,0:T(8,128)(2,1)}, u32[]{:S(2)}, u32[]{:S(2)}) %all-to-all-start.1) | async-done | bytes 2097184 | tf_op jit(solution)/shard_map/all_to_all | solution.py:86
  56.0 0.0 copy-start.1
  56.0 10.1 %all-to-all-start = ((bf16[16,16,16,256]{3,2,1,0:T(8,128)(2,1)}), bf16[16,16,16,256]{3,2,1,0:T(8,128)(2,1)S(1)}, u32[]{:S(2)}, u32[]{:S(2)}) async-start(bf16[16,16,16,256]{3,2,1,0:T(8,128)(2,1)} %bitcast.3), calls=%async_computation | async-start | bytes 4194304 | tf_op jit(solution)/shard_map/all_to_all | solution.py:87
  66.2 0.1 collective-permute-start
  66.3 0.0 copy-done.1
  66.3 0.1 reshape.24
  66.4 0.7 reshape.25.gain_ref
  67.1 3.7 %collective-permute-done = bf16[16,8,2,16,256]{4,3,2,1,0:T(8,128)(2,1)} collective-permute-done((bf16[16,8,2,16,256]{4,3,2,1,0:T(8,128)(2,1)}, bf16[16,8,2,16,256]{4,3,2,1,0:T(8,128)(2,1)}, u32[]{:S(2)}, u32[]{:S(2)}) %collective-permute-start) | collective-permute-done | bytes 2097184 | tf_op jit(solution)/shard_map/ppermute | solution.py:88
  70.8 2.5 %broadcast_select_fusion.1 = (bf16[16,8,2,16,256]{4,3,2,1,0:T(8,128)(2,1)S(1)}, bf16[16,8,2,16,256]{4,3,2,1,0:T(8,128)(2,1)S(1)}) fusion(bf16[16,8,2,16,256]{4,3,2,1,0:T(8,128)(2,1)} %all-to-all-done.1, bf16[16,8,2,16,256]{4,3,2,1,0:T(8,128)(2,1)} %collective-permute-done, pred[]{:T(512)S(6)} %eq.4), kind=kLoop, calls=%fused_computation.2 | loop fusion | flops 2097152 | bytes 8388609 | tf_op jit(solution)/shard_map/jit(_where)/select_n | solution.py:89
  73.3 2.3 %pad_maximum_fusion.filt_ref = bf16[16,16,2,16,256]{4,3,2,1,0:T(8,128)(2,1)} fusion(bf16[16,8,2,16,256]{4,3,2,1,0:T(8,128)(2,1)S(1)} %get-tuple-element.6, bf16[16,8,2,16,256]{4,3,2,1,0:T(8,128)(2,1)S(1)} %get-tuple-element.5), kind=kLoop, calls=%fused_computation | loop fusion | flops 2097152 | bytes 8388608 | tf_op jit(solution)/shard_map/concatenate | solution.py:91
  75.6 33.1 %all-to-all-done.tok_ref = bf16[16,16,16,256]{3,2,1,0:T(8,128)(2,1)S(1)} async-done(((bf16[16,16,16,256]{3,2,1,0:T(8,128)(2,1)}), bf16[16,16,16,256]{3,2,1,0:T(8,128)(2,1)S(1)}, u32[]{:S(2)}, u32[]{:S(2)}) %all-to-all-start) | async-done | bytes 2097184 | tf_op jit(solution)/shard_map/all_to_all | solution.py:87
  108.7 0.0 copy-start
  108.7 1.3 copy-done
  110.0 19.5 %shard_map.82 = bf16[16,16,16,256]{3,2,1,0:T(8,128)(2,1)} custom-call(bf16[16,16,16,256]{3,2,1,0:T(8,128)(2,1)} %copy-done, bf16[16,16,2,16,256]{4,3,2,1,0:T(8,128)(2,1)} %pad_maximum_fusion.filt_ref, f32[16]{0:T(128)} %reshape.25.gain_ref, bf16[512,256]{1,0:T(8,128)(2,1)} %constant.22.clone.first, bf16[512,512]{1,0:T(8,128)(2,1)} %constant.23.clone.forward, ...), custom_call_target="tpu_custom_call" | custom-call | tf_op jit(solution)/shard_map/pallas_call | solution.py:95
  129.5 58.0 %all_to_all.15 = bf16[16,16,16,256]{3,2,1,0:T(8,128)(2,1)S(1)} all-to-all(bf16[16,16,16,256]{3,2,1,0:T(8,128)(2,1)} %shard_map.82), channel_id=1, replica_groups=mesh['seq'=16,'bat'=2] {'seq'}, dimensions={0} | all-to-all | bytes 4194304 | tf_op jit(solution)/shard_map/all_to_all | solution.py:107
  187.5 2.3 %reshape.26 = bf16[16,2,8,4096]{3,2,1,0:T(8,128)(2,1)} reshape(bf16[16,16,16,256]{3,2,1,0:T(8,128)(2,1)S(1)} %all_to_all.15) | data formatting | bytes 4194304 | tf_op jit(solution)/shard_map/reshape | solution.py:108
  189.9 1.7 copy.15
  191.6 2.5 %copy.16 = bf16[1,4096,256]{2,1,0:T(8,128)(2,1)} copy(bf16[1,4096,256]{1,2,0:T(8,128)(2,1)S(1)} %bitcast.22) | data formatting | bytes 4194304 | tf_op jit(solution)/shard_map/broadcast_in_dim | solution.py:109
  (1 shorter events, 0.0 us)
Async XLA Ops:
  4.6 51.5 %all-to-all-start.1 = ((bf16[16,8,2,16,256]{4,3,2,1,0:T(8,128)(2,1)}), bf16[16,8,2,16,256]{4,3,2,1,0:T(8,128)(2,1)}, u32[]{:S(2)}, u32[]{:S(2)}) async-start(bf16[16,8,2,16,256]{4,3,2,1,0:T(8,128)(2,1)} %bitcast.5), calls=%async_computation.1 | async-start | bytes 4194304 | tf_op jit(solution)/shard_map/all_to_all | solution.py:86
  56.0 10.2 %copy-start.1 = (f32[256]{0:T(256)S(1)}, f32[256]{0:T(256)}, u32[]{:S(2)}) copy-start(f32[256]{0:T(256)} %param.10) | copy-start | bytes 3076
  56.0 52.6 %all-to-all-start = ((bf16[16,16,16,256]{3,2,1,0:T(8,128)(2,1)}), bf16[16,16,16,256]{3,2,1,0:T(8,128)(2,1)S(1)}, u32[]{:S(2)}, u32[]{:S(2)}) async-start(bf16[16,16,16,256]{3,2,1,0:T(8,128)(2,1)} %bitcast.3), calls=%async_computation | async-start | bytes 4194304 | tf_op jit(solution)/shard_map/all_to_all | solution.py:87
  66.2 4.6 %collective-permute-start = (bf16[16,8,2,16,256]{4,3,2,1,0:T(8,128)(2,1)}, bf16[16,8,2,16,256]{4,3,2,1,0:T(8,128)(2,1)}, u32[]{:S(2)}, u32[]{:S(2)}) collective-permute-start(bf16[16,8,2,16,256]{4,3,2,1,0:T(8,128)(2,1)} %all-to-all-done.1), channel_id=1, source_target_pairs={{0,1},{1,0},{2,3},{3,2},{4,5},{5,4},{6,7},{7,6},{8,9},{9,8},{10,11... | collective-permute-start | bytes 6291464 | tf_op jit(solution)/shard_map/ppermute | solution.py:88
  108.7 1.3 copy-start

commit v2 on v1

--- a/solution.py
+++ b/solution.py
@@ -56,23 +56,98 @@
     return (filtered + gain * tile.astype(f32)).astype(bf16)
 
 
-def kernel(tok_ref, filt_ref, gain_ref, first, forward, back, last, turn, out_ref):
-    devs, _, rows, n2 = tok_ref.shape
-    n1 = devs * rows
-    tile = tok_ref[:, 0].reshape(n1, n2)
-    filt_re = filt_ref[:, 0, 0].reshape(n1, n2)
-    filt_im = filt_ref[:, 0, 1].reshape(n1, n2)
-    gain = gain_ref[pl.program_id(0)]
-    out = convolve(
-        tile, filt_re, filt_im, gain, first[...], forward[...], back[...], last[...], turn[...]
+def kernel(
+    tok_ref, filt_ref, gain_ref, first, forward, back, last, turn, out_ref,
+    held_tok, held_filt, held_out, tok_send, tok_recv, filt_send, filt_recv,
+    pair_send, pair_recv, out_send, out_recv,
+):
+    seq = lax.axis_size("seq")
+    me, bat = lax.axis_index("seq"), lax.axis_index("bat")
+    groups, _, _, some, rows, n2 = held_tok.shape
+    part = groups * some
+    n1 = seq * rows
+    mate = (me, 1 - bat)
+    remote = functools.partial(
+        pltpu.make_async_remote_copy, device_id_type=pl.DeviceIdType.MESH
     )
-    out_ref[...] = out.reshape(devs, 1, rows, n2)
+
+    barrier = pltpu.get_barrier_semaphore()
+
+    @pl.loop(1, seq)
+    def _(k):
+        peer = (lax.rem(me + k, seq), bat)
+        pl.semaphore_signal(
+            barrier, inc=1, device_id=peer, device_id_type=pl.DeviceIdType.MESH
+        )
+
+    pl.semaphore_signal(barrier, inc=1, device_id=mate, device_id_type=pl.DeviceIdType.MESH)
+    pl.semaphore_wait(barrier, seq)
+
+    def wait_bytes(ref, sem):
+        pltpu.make_async_copy(ref, ref, sem).wait()
+
+    def pieces(g, d):
+        first_channel = d * part + g * some
+        return (
+            tok_ref.at[:, pl.ds(first_channel, some)],
+            filt_ref.at[pl.ds(first_channel, some)],
+        )
+
+    @pl.loop(0, groups)
+    def _(g):
+        tok, filt = pieces(g, me)
+        pltpu.make_async_copy(filt, held_filt.at[bat, g, me], filt_recv.at[g]).start()
+        pltpu.make_async_copy(tok, held_tok.at[g, me], tok_recv.at[g]).start()
+
+        @pl.loop(1, seq)
+        def _(k):
+            d = lax.rem(me + k, seq)
+            tok, filt = pieces(g, d)
+            remote(
+                filt, held_filt.at[bat, g, me], filt_send, filt_recv.at[g], device_id=(d, bat)
+            ).start()
+            remote(tok, held_tok.at[g, me], tok_send, tok_recv.at[g], device_id=(d, bat)).start()
+
+    @pl.loop(0, groups)
+    def _(g):
+        wait_bytes(held_filt.at[bat, g], filt_recv.at[g])
+        remote(
+            held_filt.at[bat, g], held_filt.at[bat, g], pair_send, pair_recv.at[g], device_id=mate
+        ).start()
+        wait_bytes(held_tok.at[g], tok_recv.at[g])
+        wait_bytes(held_filt.at[1 - bat, g], pair_recv.at[g])
+
+        @pl.loop(0, 2 * some)
+        def _(c):
+            h, j = c // some, lax.rem(c, some)
+            out = convolve(
+                held_tok[g, :, h, j].reshape(n1, n2),
+                held_filt[h, g, :, j, 0].reshape(n1, n2),
+                held_filt[h, g, :, j, 1].reshape(n1, n2),
+                gain_ref[h, me * part + g * some + j],
+                first[...], forward[...], back[...], last[...], turn[...],
+            )
+            held_out[g, :, h, j] = out.reshape(seq, rows, n2)
+
+        mine = out_ref.at[:, pl.ds(me * part + g * some, some)]
+        pltpu.make_async_copy(held_out.at[g, me], mine, out_recv).start()
+
+        @pl.loop(1, seq)
+        def _(k):
+            d = lax.rem(me + k, seq)
+            remote(held_out.at[g, d], mine, out_send, out_recv, device_id=(d, bat)).start()
+
+    wait_bytes(held_tok.at[:, pl.ds(0, seq - 1)], tok_send)
+    wait_bytes(held_filt.at[0, :, pl.ds(0, seq - 1)], filt_send)
+    wait_bytes(held_filt.at[0], pair_send)
+    wait_bytes(held_out.at[:, pl.ds(0, seq - 1)], out_send)
+    wait_bytes(out_ref, out_recv)
 
 
 def body(tokens, filter_spectrum, skip_gain):
     seq = lax.axis_size("seq")
     bats = lax.axis_size("bat")
-    me, bat = lax.axis_index("seq"), lax.axis_index("bat")
+    me = lax.axis_index("seq")
     sequences, local, channels = tokens.shape
     _, rows, n2, held = filter_spectrum.shape
     n1 = rows * seq
@@ -80,33 +155,30 @@
     mine = channels // seq
     if sequences == 1 and bats == 2 and held % seq == 0 and rows % 16 == 0:
         part = held // seq
-        tok = tokens[0].T.reshape(bats, seq, part, rows, n2).transpose(1, 0, 2, 3, 4)
-        tok = tok.reshape(seq, mine, rows, n2)
-        fil = filter_spectrum.transpose(3, 0, 1, 2).reshape(seq, part, 2, rows, n2)
-        fil = lax.all_to_all(fil, "seq", split_axis=0, concat_axis=0)
-        tok = lax.all_to_all(tok, "seq", split_axis=0, concat_axis=0)
-        other = lax.ppermute(fil, "bat", [(0, 1), (1, 0)])
-        low = jnp.where(bat == 0, fil, other)
-        high = jnp.where(bat == 0, other, fil)
-        fil = jnp.concatenate([low, high], axis=1)
-        gain = lax.dynamic_slice_in_dim(skip_gain.reshape(bats, seq, part), me, 1, axis=1)
-        gain = gain.reshape(mine)
-        whole = lambda t: pl.BlockSpec(t.shape, lambda c: (0,) * t.ndim)
+        some = 2 if part % 2 == 0 else 1
+        groups = part // some
+        tok = tokens[0].T.reshape(bats, held, rows, n2)
+        fil = filter_spectrum.transpose(3, 0, 1, 2)
+        hbm = pl.BlockSpec(memory_space=pltpu.HBM)
+        vmem = pl.BlockSpec(memory_space=pltpu.VMEM)
+        dma = pltpu.SemaphoreType.DMA
         out = pl.pallas_call(
             kernel,
-            grid=(mine,),
-            in_specs=[
-                pl.BlockSpec((seq, 1, rows, n2), lambda c: (0, c, 0, 0)),
-                pl.BlockSpec((seq, 1, 2, rows, n2), lambda c: (0, c, 0, 0, 0)),
-                pl.BlockSpec(memory_space=pltpu.SMEM),
-                *[whole(t) for t in consts],
+            in_specs=[hbm, hbm, pl.BlockSpec(memory_space=pltpu.SMEM), *[vmem] * len(consts)],
+            out_specs=hbm,
+            out_shape=jax.ShapeDtypeStruct((bats, held, rows, n2), jnp.bfloat16),
+            scratch_shapes=[
+                pltpu.VMEM((groups, seq, bats, some, rows, n2), jnp.bfloat16),
+                pltpu.VMEM((bats, groups, seq, some, 2, rows, n2), jnp.bfloat16),
+                pltpu.VMEM((groups, seq, bats, some, rows, n2), jnp.bfloat16),
+                dma, dma((groups,)), dma, dma((groups,)),
+                dma, dma((groups,)), dma, dma,
             ],
-            out_specs=pl.BlockSpec((seq, 1, rows, n2), lambda c: (0, c, 0, 0)),
-            out_shape=jax.ShapeDtypeStruct((seq, mine, rows, n2), jnp.bfloat16),
-        )(tok, fil, gain, *[jnp.asarray(t) for t in consts])
-        out = lax.all_to_all(out, "seq", split_axis=0, concat_axis=0)
-        out = out.reshape(seq, bats, part, local).transpose(1, 0, 2, 3).reshape(channels, local)
-        return out.T[None]
+            compiler_params=pltpu.CompilerParams(
+                collective_id=0, has_side_effects=True, vmem_limit_bytes=48 * 1024 * 1024
+            ),
+        )(tok, fil, skip_gain.reshape(bats, held), *[jnp.asarray(t) for t in consts])
+        return out.reshape(channels, local).T[None]
     fil = lax.all_gather(filter_spectrum, "bat", axis=3, tiled=True).transpose(0, 3, 1, 2)
     fil = lax.all_to_all(fil, "seq", split_axis=1, concat_axis=2, tiled=True)
     tok = tokens.reshape(sequences, rows, n2, channels).transpose(0, 3, 1, 2)

time: 195 us -> 157 us (0.81)
  Pallas kernels: 19.5 us -> 141 us
  waiting for transfers between devices: 75 us -> 0 us
  blocking collectives: 58 us -> 0 us
  starting transfers between devices: 18.6 us -> 0 us
  other arithmetic: 4.79 us -> 0 us
  local copies, waits for them, and re-layouts: 18 us -> 13.4 us
    pallas_call x1, Pallas kernels: 19.5 us -> 141 us  [body(): pl.pallas_call(kernel, in_specs=[hbm, hbm, pl.BlockSpec(memory_space=pltp...]
    all_to_all x2 -> x0, waiting for transfers between devices: 71.3 us -> none  [the longest x1 38.2 us: body(): fil = lax.all_to_all(fil, 'seq', split_axis=0, concat_axis=0)]
    all_to_all x1 -> x0, blocking collectives: 58 us -> none  [body(): out = lax.all_to_all(out, 'seq', split_axis=0, concat_axis=0)]
    all_to_all x2 -> x0, starting transfers between devices: 18.5 us -> none  [the longest x1 10.1 us: body(): tok = lax.all_to_all(tok, 'seq', split_axis=0, concat_axis=0)]
    transpose x3 -> x0, local copies, waits for them, and re-layouts: 9.44 us -> none  [the longest x2 4.89 us: body(): tokens[0].T.reshape(bats, seq, part, rows, n2).transpose(1, 0, 2, 3, 4)]
    unnamed x4 -> x14, local copies, waits for them, and re-layouts: 1.32 us -> 5.72 us
    ppermute x1 -> x0, waiting for transfers between devices: 3.7 us -> none  [body(): other = lax.ppermute(fil, 'bat', [(0, 1), (1, 0)])]
    reshape x4 -> x3, local copies, waits for them, and re-layouts: 4.79 us -> 7.72 us  [the longest x2 5.26 us: body(): tok = tokens[0].T.reshape(bats, held, rows, n2)]
  transfers between devices with their start and end apart: 3 -> 0, of which waited for: 3 -> 0; matrix products, arithmetic and copies ran while one was open for 5% -> 0% of each run, Pallas kernels for 0% -> 0%
where the time goes in v2:
time: 157 us; the launch traced here: 154 us
  Pallas kernels  141 us (90%)
  local copies, waits for them, and re-layouts  13.4 us (9%)
    pallas_call x1, Pallas kernels, body(): pl.pallas_call(kernel, in_specs=[hbm, hbm, pl.BlockSpec(memory_space=pltp...  141 us
    unnamed x14, local copies, waits for them, and re-layouts  5.72 us
    reshape x2, local copies, waits for them, and re-layouts, body(): tok = tokens[0].T.reshape(bats, held, rows, n2)  5.26 us

profile of v2, /device:TPU:0, one launch (start us, length us, event | category | flops | bytes accessed | tf_op | source)
XLA Modules:
  0.0 154.2 jit_solution(18278853041948022336)
XLA Ops:
  0.0 2.5 %reshape.12 = bf16[2,128,16,256]{1,0,3,2:T(2,128)(2,1)S(1)} reshape(bf16[256,4096]{0,1:T(8,128)(2,1)} %bitcast.17) | data formatting | bytes 4194304 | tf_op jit(solution)/shard_map/reshape | solution.py:160
  2.6 2.7 %copy.12.tok_ref = bf16[2,128,16,256]{3,2,1,0:T(8,128)(2,1)} copy(bf16[2,128,16,256]{1,0,3,2:T(2,128)(2,1)S(1)} %reshape.12) | data formatting | bytes 4194304 | tf_op jit(solution)/shard_map/reshape | solution.py:160
  5.3 0.0 copy-start
  5.3 0.0 copy-start.1
  5.3 0.0 copy-start.2
  5.3 0.0 copy-start.3
  5.3 0.0 copy-start.4
  5.3 0.0 copy-start.5
  5.3 4.8 %copy.10 = bf16[2,16,256,128]{2,1,0,3:T(8,128)(2,1)} copy(bf16[2,16,256,128]{3,2,1,0:T(8,128)(2,1)} %param.9) | data formatting | bytes 4194304 | tf_op args[1]
  10.1 0.0 copy-done
  10.1 0.0 copy-done.1
  10.1 0.0 copy-done.2
  10.1 0.0 copy-done.3
  10.1 0.0 copy-done.4
  10.1 0.0 copy-done.5
  10.1 140.7 %shard_map.82 = bf16[2,128,16,256]{3,2,1,0:T(8,128)(2,1)S(1)} custom-call(bf16[2,128,16,256]{3,2,1,0:T(8,128)(2,1)} %copy.12.tok_ref, bf16[128,2,16,256]{3,2,1,0:T(8,128)(2,1)} %bitcast.15, f32[2,128]{1,0:T(2,128)S(1)} %bitcast.14, bf16[512,256]{1,0:T(8,128)(2,1)S(1)} %copy-done.4, bf16[512,512]{1,0:T(8,128)(2,1)S(1)} %copy-done.2, ...), custom_call_target="tpu_custom_call" | custom-call | tf_op jit(solution)/shard_map/pallas_call | solution.py:165
  150.8 0.9 copy.13
  151.8 2.5 %copy.11 = bf16[256,4096]{0,1:T(8,128)(2,1)} copy(bf16[256,4096]{1,0:T(8,128)(2,1)S(1)} %bitcast.16) | data formatting | bytes 4194304 | tf_op jit(solution)/shard_map/reshape | solution.py:181
Async XLA Ops:
  5.3 4.8 %copy-start = (f32[2,256,256]{2,1,0:T(8,128)S(1)}, f32[2,256,256]{2,1,0:T(8,128)}, u32[]{:S(2)}) copy-start(f32[2,256,256]{2,1,0:T(8,128)} %constant.14.clone.turn) | copy-start | bytes 1572868
  5.3 4.8 %copy-start.1 = (bf16[512,512]{1,0:T(8,128)(2,1)S(1)}, bf16[512,512]{1,0:T(8,128)(2,1)}, u32[]{:S(2)}) copy-start(bf16[512,512]{1,0:T(8,128)(2,1)} %constant.12.clone.back) | copy-start | bytes 1572868
  5.3 4.8 %copy-start.2 = (bf16[512,512]{1,0:T(8,128)(2,1)S(1)}, bf16[512,512]{1,0:T(8,128)(2,1)}, u32[]{:S(2)}) copy-start(bf16[512,512]{1,0:T(8,128)(2,1)} %constant.11.clone.forward) | copy-start | bytes 1572868
  5.3 4.8 %copy-start.3 = (bf16[256,512]{1,0:T(8,128)(2,1)S(1)}, bf16[256,512]{1,0:T(8,128)(2,1)}, u32[]{:S(2)}) copy-start(bf16[256,512]{1,0:T(8,128)(2,1)} %constant.13.clone.last) | copy-start | bytes 786436
  5.3 4.8 %copy-start.4 = (bf16[512,256]{1,0:T(8,128)(2,1)S(1)}, bf16[512,256]{1,0:T(8,128)(2,1)}, u32[]{:S(2)}) copy-start(bf16[512,256]{1,0:T(8,128)(2,1)} %constant.10.clone.first) | copy-start | bytes 786436
  5.3 4.8 %copy-start.5 = (f32[256]{0:T(256)S(1)}, f32[256]{0:T(256)}, u32[]{:S(2)}) copy-start(f32[256]{0:T(256)} %param.10) | copy-start | bytes 3076

commit v3 on v2

--- a/solution.py
+++ b/solution.py
@@ -56,75 +56,119 @@
     return (filtered + gain * tile.astype(f32)).astype(bf16)
 
 
+def channel_major(raw, wide, turned):
+    rows, n2, lanes = raw.shape
+    tiles, _, width = wide.shape
+    step = 8
+
+    @pl.loop(0, rows)
+    def _(r):
+        flat = raw[r].astype(jnp.float32).T
+        for t in range(tiles):
+            wide[t, pl.ds(r, lanes, stride=rows), :] = flat[:, t * width : (t + 1) * width]
+
+    @pl.loop(0, lanes // step)
+    def _(q):
+        start = pl.multiple_of(q * (step * rows), step * rows)
+        for t in range(tiles):
+            block = wide[t, pl.ds(start, step * rows), :].astype(turned.dtype)
+            turned[pl.ds(q * step, step), :, t * width : (t + 1) * width] = block.reshape(
+                step, rows, width
+            )
+
+
 def kernel(
     tok_ref, filt_ref, gain_ref, first, forward, back, last, turn, out_ref,
-    held_tok, held_filt, held_out, tok_send, tok_recv, filt_send, filt_recv,
-    pair_send, pair_recv, out_send, out_recv,
+    raw_tok, raw_filt, wide, own_tok, own_filt, held_tok, held_filt, held_out,
+    load_sem, tok_send, tok_recv, filt_send, filt_recv, pair_send, pair_recv, out_send, out_recv,
 ):
     seq = lax.axis_size("seq")
     me, bat = lax.axis_index("seq"), lax.axis_index("bat")
-    groups, _, _, some, rows, n2 = held_tok.shape
+    groups, _, halves, some, rows, n2 = held_tok.shape
+    held = own_tok.shape[1]
     part = groups * some
     n1 = seq * rows
     mate = (me, 1 - bat)
-    remote = functools.partial(
-        pltpu.make_async_remote_copy, device_id_type=pl.DeviceIdType.MESH
-    )
+    mesh_id = pl.DeviceIdType.MESH
+    remote = functools.partial(pltpu.make_async_remote_copy, device_id_type=mesh_id)
+
+    loads = [pltpu.make_async_copy(filt_ref.at[p], raw_filt.at[p], load_sem.at[p]) for p in range(2)]
+    loads += [
+        pltpu.make_async_copy(
+            tok_ref.at[:, :, pl.ds(h * held, held)], raw_tok.at[h], load_sem.at[2 + h]
+        )
+        for h in range(halves)
+    ]
+    for load in loads:
+        load.start()
 
     barrier = pltpu.get_barrier_semaphore()
 
     @pl.loop(1, seq)
     def _(k):
         peer = (lax.rem(me + k, seq), bat)
-        pl.semaphore_signal(
-            barrier, inc=1, device_id=peer, device_id_type=pl.DeviceIdType.MESH
-        )
-
-    pl.semaphore_signal(barrier, inc=1, device_id=mate, device_id_type=pl.DeviceIdType.MESH)
-    pl.semaphore_wait(barrier, seq)
+        pl.semaphore_signal(barrier, inc=1, device_id=peer, device_id_type=mesh_id)
+
+    pl.semaphore_signal(barrier, inc=1, device_id=mate, device_id_type=mesh_id)
 
     def wait_bytes(ref, sem):
         pltpu.make_async_copy(ref, ref, sem).wait()
 
-    def pieces(g, d):
-        first_channel = d * part + g * some
-        return (
-            tok_ref.at[:, pl.ds(first_channel, some)],
-            filt_ref.at[pl.ds(first_channel, some)],
-        )
-
-    @pl.loop(0, groups)
-    def _(g):
-        tok, filt = pieces(g, me)
-        pltpu.make_async_copy(filt, held_filt.at[bat, g, me], filt_recv.at[g]).start()
-        pltpu.make_async_copy(tok, held_tok.at[g, me], tok_recv.at[g]).start()
+    for p in range(2):
+        loads[p].wait()
+        channel_major(raw_filt.at[p], wide, own_filt.at[p])
+        if p == 0:
+            pl.semaphore_wait(barrier, seq)
 
         @pl.loop(1, seq)
         def _(k):
             d = lax.rem(me + k, seq)
-            tok, filt = pieces(g, d)
             remote(
-                filt, held_filt.at[bat, g, me], filt_send, filt_recv.at[g], device_id=(d, bat)
+                own_filt.at[p, pl.ds(d * part, part)], held_filt.at[bat, p, me],
+                filt_send, filt_recv.at[p], device_id=(d, bat),
             ).start()
-            remote(tok, held_tok.at[g, me], tok_send, tok_recv.at[g], device_id=(d, bat)).start()
+
+        held_filt[bat, p, me] = own_filt[p, pl.ds(me * part, part)]
+
+    for h in range(halves):
+        loads[2 + h].wait()
+        channel_major(raw_tok.at[h], wide, own_tok.at[h])
 
     @pl.loop(0, groups)
     def _(g):
-        wait_bytes(held_filt.at[bat, g], filt_recv.at[g])
+        @pl.loop(1, seq)
+        def _(k):
+            d = lax.rem(me + k, seq)
+            remote(
+                own_tok.at[:, pl.ds(d * part + g * some, some)], held_tok.at[g, me],
+                tok_send, tok_recv.at[g], device_id=(d, bat),
+            ).start()
+
+        held_tok[g, me] = own_tok[:, pl.ds(me * part + g * some, some)]
+
+    others = pl.ds(0, seq - 1)
+    for p in range(2):
+        wait_bytes(held_filt.at[bat, p, others], filt_recv.at[p])
         remote(
-            held_filt.at[bat, g], held_filt.at[bat, g], pair_send, pair_recv.at[g], device_id=mate
+            held_filt.at[bat, p], held_filt.at[bat, p], pair_send.at[p], pair_recv.at[p],
+            device_id=mate,
         ).start()
-        wait_bytes(held_tok.at[g], tok_recv.at[g])
-        wait_bytes(held_filt.at[1 - bat, g], pair_recv.at[g])
-
-        @pl.loop(0, 2 * some)
+    for p in range(2):
+        wait_bytes(held_filt.at[1 - bat, p], pair_recv.at[p])
+
+    @pl.loop(0, groups)
+    def _(g):
+        wait_bytes(held_tok.at[g, others], tok_recv.at[g])
+
+        @pl.loop(0, halves * some)
         def _(c):
             h, j = c // some, lax.rem(c, some)
+            channel = g * some + j
             out = convolve(
                 held_tok[g, :, h, j].reshape(n1, n2),
-                held_filt[h, g, :, j, 0].reshape(n1, n2),
-                held_filt[h, g, :, j, 1].reshape(n1, n2),
-                gain_ref[h, me * part + g * some + j],
+                held_filt[h, 0, :, channel].reshape(n1, n2),
+                held_filt[h, 1, :, channel].reshape(n1, n2),
+                gain_ref[h, me * part + channel],
                 first[...], forward[...], back[...], last[...], turn[...],
             )
             held_out[g, :, h, j] = out.reshape(seq, rows, n2)
@@ -137,10 +181,11 @@
             d = lax.rem(me + k, seq)
             remote(held_out.at[g, d], mine, out_send, out_recv, device_id=(d, bat)).start()
 
-    wait_bytes(held_tok.at[:, pl.ds(0, seq - 1)], tok_send)
-    wait_bytes(held_filt.at[0, :, pl.ds(0, seq - 1)], filt_send)
-    wait_bytes(held_filt.at[0], pair_send)
-    wait_bytes(held_out.at[:, pl.ds(0, seq - 1)], out_send)
+    wait_bytes(held_tok.at[:, others], tok_send)
+    wait_bytes(held_filt.at[0, :, others], filt_send)
+    for p in range(2):
+        wait_bytes(held_filt.at[bat, p], pair_send.at[p])
+    wait_bytes(held_out.at[:, others], out_send)
     wait_bytes(out_ref, out_recv)
 
 
@@ -153,31 +198,37 @@
     n1 = rows * seq
     consts = tables(n1, n2)
     mine = channels // seq
-    if sequences == 1 and bats == 2 and held % seq == 0 and rows % 16 == 0:
+    lane = 128
+    if sequences == 1 and bats == 2 and held % seq == 0 and rows % 16 == 0 and held % lane == 0 and n2 % lane == 0:
         part = held // seq
         some = 2 if part % 2 == 0 else 1
         groups = part // some
-        tok = tokens[0].T.reshape(bats, held, rows, n2)
-        fil = filter_spectrum.transpose(3, 0, 1, 2)
+        tok = tokens.reshape(rows, n2, channels)
         hbm = pl.BlockSpec(memory_space=pltpu.HBM)
         vmem = pl.BlockSpec(memory_space=pltpu.VMEM)
         dma = pltpu.SemaphoreType.DMA
+        half = lambda shape: pltpu.VMEM(shape, jnp.bfloat16)
         out = pl.pallas_call(
             kernel,
             in_specs=[hbm, hbm, pl.BlockSpec(memory_space=pltpu.SMEM), *[vmem] * len(consts)],
             out_specs=hbm,
             out_shape=jax.ShapeDtypeStruct((bats, held, rows, n2), jnp.bfloat16),
             scratch_shapes=[
-                pltpu.VMEM((groups, seq, bats, some, rows, n2), jnp.bfloat16),
-                pltpu.VMEM((bats, groups, seq, some, 2, rows, n2), jnp.bfloat16),
-                pltpu.VMEM((groups, seq, bats, some, rows, n2), jnp.bfloat16),
-                dma, dma((groups,)), dma, dma((groups,)),
-                dma, dma((groups,)), dma, dma,
+                half((bats, rows, n2, held)),
+                half((2, rows, n2, held)),
+                pltpu.VMEM((n2 // lane, held * rows, lane), jnp.float32),
+                half((bats, held, rows, n2)),
+                half((2, held, rows, n2)),
+                half((groups, seq, bats, some, rows, n2)),
+                half((bats, 2, seq, part, rows, n2)),
+                half((groups, seq, bats, some, rows, n2)),
+                dma((2 + bats,)), dma, dma((groups,)), dma, dma((2,)),
+                dma((2,)), dma((2,)), dma, dma,
             ],
             compiler_params=pltpu.CompilerParams(
                 collective_id=0, has_side_effects=True, vmem_limit_bytes=48 * 1024 * 1024
             ),
-        )(tok, fil, skip_gain.reshape(bats, held), *[jnp.asarray(t) for t in consts])
+        )(tok, filter_spectrum, skip_gain.reshape(bats, held), *[jnp.asarray(t) for t in consts])
         return out.reshape(channels, local).T[None]
     fil = lax.all_gather(filter_spectrum, "bat", axis=3, tiled=True).transpose(0, 3, 1, 2)
     fil = lax.all_to_all(fil, "seq", split_axis=1, concat_axis=2, tiled=True)

time: 157 us -> 152 us (0.968); the launches traced: 154 us -> 152 us
  local copies, waits for them, and re-layouts: 13.4 us -> 9.13 us
  Pallas kernels: 141 us -> 143 us
    reshape x2 -> x0, local copies, waits for them, and re-layouts: 5.26 us -> none  [body(): tok = tokens[0].T.reshape(bats, held, rows, n2)]
    pallas_call x1, Pallas kernels: 141 us -> 143 us  [body(): pl.pallas_call(kernel, in_specs=[hbm, hbm, pl.BlockSpec(memory_space=pltp...]
    unnamed x14 -> x13, local copies, waits for them, and re-layouts: 5.72 us -> 6.68 us
where the time goes in v3:
time: 152 us
  Pallas kernels  143 us (94%)
  local copies, waits for them, and re-layouts  9.13 us (6%)
    pallas_call x1, Pallas kernels, body(): pl.pallas_call(kernel, in_specs=[hbm, hbm, pl.BlockSpec(memory_space=pltp...  143 us
    unnamed x13, local copies, waits for them, and re-layouts  6.68 us

profile of v3, /device:TPU:0, one launch (start us, length us, event | category | flops | bytes accessed | tf_op | source)
XLA Modules:
  0.0 151.7 jit_solution(5943993406331653321)
XLA Ops:
  0.0 0.0 copy-start
  0.0 1.0 copy-done
  1.0 0.0 copy-start.1
  1.0 1.0 copy-done.1
  2.1 0.0 copy-start.2
  2.1 1.0 copy-done.2
  3.1 0.0 copy-start.3
  3.1 0.9 copy-done.3
  4.1 0.0 copy-start.4
  4.1 0.9 copy-done.4
  5.0 0.0 copy-start.5
  5.0 0.7 copy-done.5
  5.7 142.6 %shard_map.82 = bf16[2,128,16,256]{3,2,1,0:T(8,128)(2,1)S(1)} custom-call(bf16[16,256,256]{2,1,0:T(8,128)(2,1)} %bitcast.11, bf16[2,16,256,128]{3,2,1,0:T(8,128)(2,1)} %filt_ref.1, f32[2,128]{1,0:T(2,128)S(1)} %bitcast.9, bf16[512,256]{1,0:T(8,128)(2,1)S(1)} %copy-done.4, bf16[512,512]{1,0:T(8,128)(2,1)S(1)} %copy-done.2, bf16[512,512]{1,0:T(8,128)(2,1)S(1)} %copy-done.1, ...), custom_call_target="tpu_custom_call" | custom-call | tf_op jit(solution)/shard_map/pallas_call | solution.py:211
  148.3 1.0 copy.10
  149.3 2.5 %copy.9 = bf16[256,4096]{0,1:T(8,128)(2,1)} copy(bf16[256,4096]{1,0:T(8,128)(2,1)S(1)} %bitcast.10) | data formatting | bytes 4194304 | tf_op jit(solution)/shard_map/reshape | solution.py:232
Async XLA Ops:
  0.0 1.0 copy-start
  1.0 1.0 copy-start.1
  2.1 1.0 copy-start.2
  3.1 0.9 copy-start.3
  4.1 0.9 copy-start.4
  5.0 0.7 copy-start.5

commit v4 on v3

--- a/solution.py
+++ b/solution.py
@@ -77,11 +77,13 @@
             )
 
 
-def kernel(
-    tok_ref, filt_ref, gain_ref, first, forward, back, last, turn, out_ref,
-    raw_tok, raw_filt, wide, own_tok, own_filt, held_tok, held_filt, held_out,
-    load_sem, tok_send, tok_recv, filt_send, filt_recv, pair_send, pair_recv, out_send, out_recv,
-):
+def kernel(tok_ref, filt_ref, gain_ref, *refs):
+    table_refs, refs = refs[:5], refs[5:]
+    out_ref, table_bufs, refs = refs[0], refs[1:6], refs[6:]
+    raw_tok, raw_filt, wide, own_tok, own_filt, held_tok, held_filt, held_out = refs[:8]
+    load_sem, table_sem, tok_send, tok_recv, filt_send, filt_recv = refs[8:14]
+    pair_send, pair_recv, out_send, out_recv = refs[14:]
+    first, forward, back, last, turn = table_bufs
     seq = lax.axis_size("seq")
     me, bat = lax.axis_index("seq"), lax.axis_index("bat")
     groups, _, halves, some, rows, n2 = held_tok.shape
@@ -99,7 +101,11 @@
         )
         for h in range(halves)
     ]
-    for load in loads:
+    table_loads = [
+        pltpu.make_async_copy(src, dst, table_sem.at[i])
+        for i, (src, dst) in enumerate(zip(table_refs, table_bufs))
+    ]
+    for load in loads + table_loads:
         load.start()
 
     barrier = pltpu.get_barrier_semaphore()
@@ -145,6 +151,9 @@
             ).start()
 
         held_tok[g, me] = own_tok[:, pl.ds(me * part + g * some, some)]
+
+    for load in table_loads:
+        load.wait()
 
     others = pl.ds(0, seq - 1)
     for p in range(2):
@@ -205,15 +214,15 @@
         groups = part // some
         tok = tokens.reshape(rows, n2, channels)
         hbm = pl.BlockSpec(memory_space=pltpu.HBM)
-        vmem = pl.BlockSpec(memory_space=pltpu.VMEM)
         dma = pltpu.SemaphoreType.DMA
         half = lambda shape: pltpu.VMEM(shape, jnp.bfloat16)
         out = pl.pallas_call(
             kernel,
-            in_specs=[hbm, hbm, pl.BlockSpec(memory_space=pltpu.SMEM), *[vmem] * len(consts)],
+            in_specs=[hbm, hbm, pl.BlockSpec(memory_space=pltpu.SMEM), *[hbm] * len(consts)],
             out_specs=hbm,
             out_shape=jax.ShapeDtypeStruct((bats, held, rows, n2), jnp.bfloat16),
             scratch_shapes=[
+                *[pltpu.VMEM(t.shape, t.dtype) for t in consts],
                 half((bats, rows, n2, held)),
                 half((2, rows, n2, held)),
                 pltpu.VMEM((n2 // lane, held * rows, lane), jnp.float32),
@@ -222,11 +231,11 @@
                 half((groups, seq, bats, some, rows, n2)),
                 half((bats, 2, seq, part, rows, n2)),
                 half((groups, seq, bats, some, rows, n2)),
-                dma((2 + bats,)), dma, dma((groups,)), dma, dma((2,)),
+                dma((2 + bats,)), dma((len(consts),)), dma, dma((groups,)), dma, dma((2,)),
                 dma((2,)), dma((2,)), dma, dma,
             ],
             compiler_params=pltpu.CompilerParams(
-                collective_id=0, has_side_effects=True, vmem_limit_bytes=48 * 1024 * 1024
+                collective_id=0, has_side_effects=True, vmem_limit_bytes=66_900_000
             ),
         )(tok, filter_spectrum, skip_gain.reshape(bats, held), *[jnp.asarray(t) for t in consts])
         return out.reshape(channels, local).T[None]

time: 152 us -> 148 us (0.974)
  local copies, waits for them, and re-layouts: 9.13 us -> 4.98 us
    unnamed x13 -> x1, local copies, waits for them, and re-layouts: 6.68 us -> 2.53 us
where the time goes in v4:
time: 148 us
  Pallas kernels  143 us (97%)
  local copies, waits for them, and re-layouts  4.98 us (3%)
    pallas_call x1, Pallas kernels, body(): pl.pallas_call(kernel, in_specs=[hbm, hbm, pl.BlockSpec(memory_space=pltp...  143 us

profile of v4, /device:TPU:0, one launch (start us, length us, event | category | flops | bytes accessed | tf_op | source)
XLA Modules:
  0.0 147.9 jit_solution(16313779450929776041)
XLA Ops:
  0.0 142.9 %shard_map.82 = bf16[2,128,16,256]{3,2,1,0:T(8,128)(2,1)} custom-call(bf16[16,256,256]{2,1,0:T(8,128)(2,1)} %bitcast.10, bf16[2,16,256,128]{3,2,1,0:T(8,128)(2,1)} %filt_ref.1, f32[2,128]{1,0:T(2,128)} %bitcast.11, bf16[512,256]{1,0:T(8,128)(2,1)} %constant.10.clone.refs_0_, bf16[512,512]{1,0:T(8,128)(2,1)} %constant.11.clone.refs_1_, ...), custom_call_target="tpu_custom_call" | custom-call | tf_op jit(solution)/shard_map/pallas_call | solution.py:219
  143.0 2.5 %copy.10 = bf16[32,8,16,256]{3,1,2,0:T(8,128)(2,1)S(1)} copy(bf16[32,8,16,256]{3,2,1,0:T(8,128)(2,1)} %bitcast.8) | data formatting | bytes 4194304
  145.5 2.5 %copy.9 = bf16[256,4096]{0,1:T(8,128)(2,1)} copy(bf16[256,4096]{1,0:T(8,128)(2,1)S(1)} %bitcast.9) | data formatting | bytes 4194304 | tf_op jit(solution)/shard_map/reshape | solution.py:241
